TPU v7x, 512 devices: a whole 4x4x16 slice. The times are simulated.
512 devices in a mesh: harm: 32 (over z, x_hi), slab: 16 (over y, x_lo, core).
Axes of the slice: x: 4 (x_hi: 2, x_lo: 2; x = x_hi * 2 + x_lo), y: 4, z: 16, core: 2. Of those that a mesh axis runs over, the one named last changes fastest.
Arguments:
- harmonics: float32 [32, 2, 5, 32, 2048], P('harm', None, None, 'slab'), may hold values from -4 to 4
- mean_flow: float32 [5, 32, 2048], P(None, 'slab'), may hold values from 0.5 to 13.5
- freq_index: int32 [32], P('harm'), may hold values from 1 to 8
- wall_mask: int32 [32, 2048], P('slab'), may hold values 0 or 1
- jacobian_x: float32 [5, 5], replicated, may hold values from -2.5 to 2.5
- jacobian_y: float32 [5, 5], replicated, may hold values from -2.5 to 2.5
Outputs:
- mean_next: float32 [5, 32, 2048], P(None, 'slab')
- harmonics_next: float32 [32, 2, 5, 32, 2048], P('harm', None, None, 'slab')
All inputs are finite; a program needn't handle non-finite values. No bound on the sum of `wall_mask` on one device may be relied on, other than what follows from the above.
Results may differ from a plain program's by a relative error of at most 0.00018.
Values sent between devices are 32-bit elements; how exact they have to be, the bound alone decides.
No kernel may reach another device: no remote copies, remote signals or barrier semaphores. Data moves between devices by JAX's collectives and lax.ppermute only.
A program may use at most 64 MiB of HBM per device.

v0:
```python
import functools

import jax
import jax.numpy as jnp
from jax import lax
from jax.experimental import pallas as pl
from jax.experimental.pallas import tpu as pltpu
from jax.sharding import PartitionSpec as P


NZ = 64
EPS_FOURTH = 0.05
COURANT = 0.9
OMEGA_BASE = 0.25
WALL_RATE = 2.0
HUB_RADIUS = 0.5
SECTION_RATES = (0.25, 1.0 / 3.0, 0.5, 1.0)
STRESS_PAIRS = ((1, 1), (1, 2), (1, 3), (2, 2), (2, 3), (3, 3), (4, 1), (4, 2), (4, 3))

VARS = 5
CELLS = 2
C1 = 16
LANES = 128
H_ROWS = 2 * VARS * CELLS * C1
M_ROWS = VARS * CELLS * C1
W_ROWS = CELLS * C1


def h_row(part, var, cell):
    return ((part * VARS + var) * CELLS + cell) * C1


def m_row(var, cell):
    return (var * CELLS + cell) * C1


def pack_mean(tiles):
    group = lax.broadcasted_iota(jnp.int32, (8, LANES), 1) // 4
    packed = jnp.zeros((8, LANES), jnp.float32)
    for i, tile in enumerate(tiles):
        for half in range(2):
            packed = jnp.where(group == 2 * i + half, tile[8 * half : 8 * half + 8, :], packed)
    return packed


def unpack_mean(packed):
    lane = lax.broadcasted_iota(jnp.int32, (8, LANES), 1) % 4
    tiles = []
    for i in range(VARS * CELLS):
        halves = [
            jnp.take_along_axis(packed, lane + 4 * (2 * i + half), axis=1) for half in range(2)
        ]
        tiles.append(jnp.concatenate(halves, axis=0))
    return tiles


def open_kernel(
    harm_ref, mean_ref, wall_ref, jac_x_ref, jac_y_ref, freq_ref, position_ref,
    out_ref, mean_out, wall_out, packed_out, speed_out, jac_out, radius_out,
    rows_ref, plane_ref
):
    for cell in range(CELLS):
        for c1 in range(C1):
            cols = slice(c1 * LANES, (c1 + 1) * LANES)
            for var in range(VARS):
                for part in range(2):
                    row = h_row(part, var, cell) + c1
                    rows_ref[row : row + 1, :] = harm_ref[0, part, var, cell : cell + 1, cols]
                row = m_row(var, cell) + c1
                plane_ref[row : row + 1, :] = mean_ref[var, cell : cell + 1, cols]
            row = M_ROWS + cell * C1 + c1
            plane_ref[row : row + 1, :] = wall_ref[cell : cell + 1, cols].astype(jnp.float32)
    omega = OMEGA_BASE * freq_ref[0].astype(jnp.float32)
    rows_ref[H_ROWS:, :] = jnp.full((rows_ref.shape[0] - H_ROWS, LANES), omega, jnp.float32)
    turned = rows_ref[...].T
    for j in range(32):
        out_ref[j, 0:2, :] = turned[2 * j : 2 * j + 2, :]
        out_ref[j, 2:4, :] = turned[NZ + 2 * j : NZ + 2 * j + 2, :]

    for base, matrix_ref in ((0, jac_x_ref), (VARS * VARS, jac_y_ref)):
        for a in range(VARS):
            for b in range(VARS):
                row = base + VARS * a + b
                jac_out[row : row + 1, :] = jnp.broadcast_to(
                    matrix_ref[a : a + 1, b : b + 1], (1, LANES)
                )
    lane = lax.broadcasted_iota(jnp.int32, (8, LANES), 1)
    radial = 2 * position_ref[0] + lane % 2
    radius_out[...] = HUB_RADIUS + (radial.astype(jnp.float32) + 0.5) / NZ
    source = ((lane // 2) % 2) * NZ + radial
    for start in range(0, M_ROWS + W_ROWS, 8):
        picked = jnp.take_along_axis(plane_ref[start : start + 8, :], source, axis=1)
        if start < M_ROWS:
            mean_out[start : start + 8, :] = picked
        else:
            wall_out[start - M_ROWS : start - M_ROWS + 8, :] = picked
    momentum = plane_ref[m_row(1, 0) : m_row(2, 0), :]
    speed_out[...] = jnp.full(speed_out.shape, jnp.sum(momentum * momentum), jnp.float32)
    packed_out[...] = pack_mean(
        [mean_out[i * C1 : (i + 1) * C1, :] for i in range(VARS * CELLS)]
    )


def unpack_kernel(arrived_ref, packed_ref, state_out, omega_out, rows_ref):
    for k in range(32):
        rows_ref[4 * k : 4 * k + 4, :] = arrived_ref[k]
    turned = rows_ref[...].T
    state_out[:H_ROWS, :] = turned[:H_ROWS, :]
    state_out[H_ROWS:, :] = packed_ref[...]
    omega_out[...] = turned[H_ROWS : H_ROWS + 8, :]


def section_kernel(*refs, stage, cell_count):
    last = stage == len(SECTION_RATES) - 1
    parity_ref, own_ref, core_ref, chip_ref, *refs = refs
    mean_ref, omega_ref, wall_ref, jac_ref, radius_ref, *refs = refs
    if stage == 0:
        outs = refs
    elif stage == 1:
        speed_ref, own_res, core_res, chip_res, mean_res, *outs = refs
        h0_ref, m0_ref = own_ref, mean_ref
    else:
        speed_ref, h0_ref, m0_ref, *outs = refs
    lane = lax.broadcasted_iota(jnp.int32, (C1, LANES), 1)
    even = (lane // 2) % 2 == 0

    def up(tile):
        return pltpu.roll(tile, C1 - 1, 0)

    def down(tile):
        return pltpu.roll(tile, 1, 0)

    def beside(tile):
        swapped = jnp.where(even, pltpu.roll(tile, LANES - 2, 1), pltpu.roll(tile, 2, 1))
        return jnp.where(even, swapped, up(swapped)), jnp.where(even, down(swapped), swapped)

    def splat(ref, row):
        return jnp.broadcast_to(ref[row : row + 1, :], (C1, LANES))

    def apply_matrix(base, tiles):
        out = []
        for a in range(VARS):
            total = splat(jac_ref, base + VARS * a) * tiles[0]
            for b in range(1, VARS):
                total = total + splat(jac_ref, base + VARS * a + b) * tiles[b]
            out.append(total)
        return out

    omega = splat(omega_ref, 0)
    if stage:
        speed_total = jnp.sum(speed_ref[...], axis=0)
        time_step = COURANT / (1.0 + jnp.sqrt(speed_total / cell_count))
        time_step = jnp.broadcast_to(time_step, (C1, LANES))
        step = SECTION_RATES[stage] * time_step
    own, core, chip = (own_ref, None), (core_ref, None), (chip_ref, None)
    mean_block = (mean_ref, None)
    if stage == 1:
        first = SECTION_RATES[0] * time_step
        own, core, chip = (own_ref, own_res), (core_ref, core_res), (chip_ref, chip_res)
        mean_block = (mean_ref, mean_res)

    def load(block, row, count=C1):
        base, residual = block
        value = base[row : row + count, :]
        if residual is not None:
            value = value + first[:count] * residual[row : row + count, :]
        return value

    on_first = parity_ref[0] == 0

    def sides(row, count=C1):
        paired, other = load(core, row, count), load(chip, row, count)
        return jnp.where(on_first, other, paired), jnp.where(on_first, paired, other)

    def column(part, var):
        rows = [h_row(part, var, cell) for cell in range(CELLS)]
        left, right = zip(*[sides(row) for row in rows])
        return [*left, *[load(own, row) for row in rows], *right]

    inv_radius = 1.0 / splat(radius_ref, 0)

    harm = [[column(part, var) for var in range(VARS)] for part in range(2)]
    left_mean, right_mean = [unpack_mean(packed) for packed in sides(H_ROWS, 8)]
    mean = []
    for var in range(VARS):
        own_mean = [load(mean_block, m_row(var, cell)) for cell in range(CELLS)]
        mean.append(
            left_mean[CELLS * var : CELLS * (var + 1)]
            + own_mean
            + right_mean[CELLS * var : CELLS * (var + 1)]
        )

    def smooth_parts(cells, at):
        center = cells[at]
        above, below = beside(center)
        diff_y = (above - below) * 0.5
        fourth = (
            (cells[at + 2] + cells[at - 2])
            + (up(center) + down(center))
            - 4.0 * ((cells[at + 1] + cells[at - 1]) + (above + below))
            + 12.0 * center
        )
        return diff_y, fourth

    harm_new = {}
    for cell in range(CELLS):
        at = 2 + cell
        wall = WALL_RATE * wall_ref[cell * C1 : (cell + 1) * C1, :]
        for part in range(2):
            diffs_x, diffs_y, fourths = [], [], []
            for var in range(VARS):
                cells = harm[part][var]
                diffs_x.append(
                    (mean[1][at + 1] * cells[at + 1] - mean[1][at - 1] * cells[at - 1]) * 0.5
                )
                diff_y, fourth = smooth_parts(cells, at)
                diffs_y.append(diff_y)
                fourths.append(fourth)
            flux_x = apply_matrix(0, diffs_x)
            flux_y = apply_matrix(VARS * VARS, diffs_y)
            for var in range(VARS):
                turned = omega * harm[1 - part][var][at]
                if part:
                    turned = -turned
                res = (
                    turned
                    - flux_x[var]
                    - flux_y[var]
                    - EPS_FOURTH * fourths[var]
                    - wall * harm[part][var][at]
                )
                row = h_row(part, var, cell)
                if stage:
                    res = h0_ref[row : row + C1, :] + step * res
                harm_new[part, var, cell] = res

    def stress(index, at):
        a, b = STRESS_PAIRS[index]
        return 0.5 * (harm[0][a][at] * harm[0][b][at] + harm[1][a][at] * harm[1][b][at])

    def total(tile):
        for shift in (4, 8, 16, 32, 64):
            tile = tile + pltpu.roll(tile, shift, 1)
        return jnp.take_along_axis(tile, lane % 4, axis=1)

    mean_new = {}
    for cell in range(CELLS):
        at = 2 + cell

        def grad_x(index):
            return (stress(index, at + 1) - stress(index, at - 1)) * 0.5

        def grad_y(tile):
            above, below = beside(tile)
            return (above - below) * 0.5

        s3, s4 = stress(3, at), stress(4, at)
        terms = [
            None,
            total(-grad_x(0) - grad_y(stress(1, at))),
            total(-grad_x(1) - grad_y(s3) - 2.0 * s4 * inv_radius),
            total(-grad_x(2) - grad_y(s4) + (s3 - stress(5, at)) * inv_radius),
            total(-grad_x(6) - grad_y(stress(7, at)) - stress(8, at) * inv_radius),
        ]
        diffs_x, diffs_y, fourths = [], [], []
        for var in range(VARS):
            cells = mean[var]
            diffs_x.append((cells[at + 1] - cells[at - 1]) * 0.5)
            diff_y, fourth = smooth_parts(cells, at)
            diffs_y.append(diff_y)
            fourths.append(fourth)
        flux_x = apply_matrix(0, diffs_x)
        flux_y = apply_matrix(VARS * VARS, diffs_y)
        for var in range(VARS):
            res = -flux_x[var] - flux_y[var] - EPS_FOURTH * fourths[var]
            if var:
                res = res + terms[var]
            row = m_row(var, cell)
            if stage:
                res = m0_ref[row : row + C1, :] + step * res
            mean_new[var, cell] = res

    if last:
        out_ref, rows_ref = outs
        target, offset = rows_ref, H_ROWS
    else:
        state_out, mean_out = outs
        target, offset = state_out, None
    for (part, var, cell), tile in harm_new.items():
        row = h_row(part, var, cell)
        target[row : row + C1, :] = tile
    for (var, cell), tile in mean_new.items():
        row = m_row(var, cell)
        if last:
            target[offset + row : offset + row + C1, :] = tile
        else:
            mean_out[row : row + C1, :] = tile
    if last:
        spare = H_ROWS + M_ROWS
        rows_ref[spare:, :] = jnp.zeros((rows_ref.shape[0] - spare, LANES), jnp.float32)
        turned = rows_ref[...].T
        for k in range(32):
            out_ref[k] = turned[4 * k : 4 * k + 4, :]
    else:
        state_out[H_ROWS:, :] = pack_mean(
            [mean_new[var, cell] for var in range(VARS) for cell in range(CELLS)]
        )


def restore_kernel(arrived_ref, mean_out, harm_out, rows_ref):
    for j in range(32):
        rows_ref[2 * j : 2 * j + 2, :] = arrived_ref[j, 0:2, :]
        rows_ref[NZ + 2 * j : NZ + 2 * j + 2, :] = arrived_ref[j, 2:4, :]
    turned = rows_ref[...].T
    for var in range(VARS):
        for cell in range(CELLS):
            for c1 in range(C1):
                cols = slice(c1 * LANES, (c1 + 1) * LANES)
                for part in range(2):
                    row = h_row(part, var, cell) + c1
                    harm_out[0, part, var, cell : cell + 1, cols] = turned[row : row + 1, :]
                row = H_ROWS + m_row(var, cell) + c1
                mean_out[var, cell : cell + 1, cols] = turned[row : row + 1, :]


def f32(*shape):
    return jax.ShapeDtypeStruct(shape, jnp.float32)


def kept(*shape):
    return pltpu.VMEM(shape, jnp.float32)


def held(*arrays):
    return [pltpu.with_memory_space_constraint(array, pltpu.VMEM) for array in arrays]


VMEM = pl.BlockSpec(memory_space=pltpu.VMEM)
SMEM = pl.BlockSpec(memory_space=pltpu.SMEM)


def rows_scratch(*shape):
    return [pltpu.VMEM(shape, jnp.float32)]


def shards(harmonics, mean_flow, freq_index, wall_mask, jacobian_x, jacobian_y):
    plane_count = mean_flow.shape[2]
    slab_count = lax.axis_size("slab")
    position = lax.axis_index("harm")

    sends, mean_start, wall, packed, speed, jac, radius = pl.pallas_call(
        open_kernel,
        out_shape=(
            kept(32, 4, 384),
            kept(M_ROWS, LANES),
            kept(W_ROWS, LANES),
            kept(8, LANES),
            kept(slab_count, 1, LANES),
            kept(2 * VARS * VARS, LANES),
            kept(8, LANES),
        ),
        in_specs=[VMEM] * 5 + [SMEM] * 2,
        out_specs=(VMEM,) * 7,
        scratch_shapes=rows_scratch(384, LANES) + rows_scratch(M_ROWS + W_ROWS, LANES),
        name="open",
    )(
        harmonics, mean_flow, wall_mask, jacobian_x, jacobian_y, freq_index,
        position.astype(jnp.int32).reshape(1),
    )
    arrived = lax.all_to_all(sends, "harm", 0, 0, tiled=True)
    start, omega = pl.pallas_call(
        unpack_kernel,
        out_shape=(kept(H_ROWS + 8, LANES), kept(8, LANES)),
        in_specs=[VMEM] * 2,
        out_specs=(VMEM,) * 2,
        scratch_shapes=rows_scratch(LANES, 384),
        name="unpack",
    )(*held(arrived, packed))

    omega, speed = lax.optimization_barrier((omega, speed))
    speeds = lax.all_to_all(speed, "slab", 0, 0, tiled=True)
    cell_count = CELLS * slab_count * plane_count

    core_pairs = [(i, i ^ 1) for i in range(slab_count)]
    chip_pairs = [
        pair for i in range(1, slab_count - 1, 2) for pair in ((i, i + 1), (i + 1, i))
    ]

    def beside(state):
        core = lax.ppermute(state, "slab", core_pairs)
        chip = lax.ppermute(state, "slab", chip_pairs)
        return state, core, chip

    def section(stage, *operands):
        if stage == len(SECTION_RATES) - 1:
            shapes, scratch = kept(32, 4, 512), rows_scratch(512, LANES)
            specs = VMEM
        else:
            shapes, scratch = (kept(H_ROWS + 8, LANES), kept(M_ROWS, LANES)), []
            specs = (VMEM, VMEM)
        return pl.pallas_call(
            functools.partial(section_kernel, stage=stage, cell_count=cell_count),
            out_shape=shapes,
            in_specs=[SMEM] + [VMEM] * len(operands),
            out_specs=specs,
            scratch_shapes=scratch,
        )(parity, *held(*operands))

    parity = (lax.axis_index("slab") % 2).astype(jnp.int32).reshape(1)
    fixed = (omega, wall, jac, radius)
    start_blocks = beside(start)
    residual, mean_residual = section(0, *start_blocks, mean_start, *fixed)
    state, mean_now = section(
        1, *start_blocks, mean_start, *fixed, speeds, *beside(residual), mean_residual
    )
    state, mean_now = section(2, *beside(state), mean_now, *fixed, speeds, start, mean_start)
    result = section(3, *beside(state), mean_now, *fixed, speeds, start, mean_start)
    back = lax.all_to_all(result, "harm", 0, 0, tiled=True)
    return pl.pallas_call(
        restore_kernel,
        out_shape=(f32(*mean_flow.shape), f32(*harmonics.shape)),
        in_specs=[VMEM],
        out_specs=(VMEM, VMEM),
        scratch_shapes=rows_scratch(LANES, 512),
        name="restore",
    )(*held(back))


def solution(mesh):
    placed = (
        P("harm", None, None, "slab", None),
        P(None, "slab", None),
        P("harm"),
        P("slab", None),
        P(),
        P(),
    )
    return jax.shard_map(
        shards,
        mesh=mesh,
        in_specs=placed,
        out_specs=(P(None, "slab", None), P("harm", None, None, "slab", None)),
        check_vma=False,
    )
```

profile of v0, /device:TPU:7, one launch (start us, length us, event | category | flops | bytes accessed | tf_op | source)
XLA Modules:
  0.0 109.8 jit_solution(4132010145947197235)
XLA Ops:
  1.3 1.3 %open.1 = (f32[32,4,384]{2,1,0:T(4,128)S(1)}, f32[160,128]{1,0:T(8,128)S(1)}, f32[32,128]{1,0:T(8,128)S(1)}, f32[8,128]{1,0:T(8,128)S(1)}, f32[16,1,128]{2,1,0:T...) custom-call(f32[1,2,5,2,2048]{4,3,2,1,0:T(2,128)} %harm_ref.1, f32[5,2,2048]{2,1,0:T(2,128)} %mean_ref.1, ...), custom_call_target="tpu_custom_call" | custom-call | tf_op jit(solution)/shard_map/open/pallas_call | solution.py:351
  2.6 34.5 %all_to_all.15.arrived_ref = f32[32,4,384]{2,1,0:T(4,128)S(1)} all-to-all(f32[32,4,384]{2,1,0:T(4,128)S(1)} %get-tuple-element.19), channel_id=1, replica_groups=mesh['harm'=32,'slab'=16] {'harm'}, dimensions={0} | all-to-all | bytes 393216 | tf_op jit(solution)/shard_map/all_to_all | solution.py:370
  37.1 0.1 unpack.1
  37.3 6.3 %collective-permute-start.1 = (f32[328,128]{1,0:T(8,128)S(1)}, f32[328,128]{1,0:T(8,128)S(1)}, u32[]{:S(2)}, u32[]{:S(2)}) collective-permute-start(f32[328,128]{1,0:T(8,128)S(1)} %get-tuple-element.21.refs_1_.refs_10_), channel_id=1, source_target_pairs={{1,2},{2,1},{3,4},{4,3},{5,6},{6,5},{7,8},{8,7},{9,10},{10,9},{11,... | collective-permute-start | bytes 503816 | tf_op jit(solution)/shard_map/ppermute | solution.py:391
  43.5 1.9 %collective-permute-start = (f32[328,128]{1,0:T(8,128)S(1)}, f32[328,128]{1,0:T(8,128)S(1)}, u32[]{:S(2)}, u32[]{:S(2)}) collective-permute-start(f32[328,128]{1,0:T(8,128)S(1)} %get-tuple-element.21.refs_1_.refs_10_), channel_id=1, source_target_pairs={{0,1},{1,0},{2,3},{3,2},{4,5},{5,4},{6,7},{7,6},{8,9},{9,8},{10,11... | collective-permute-start | bytes 503816 | tf_op jit(solution)/shard_map/ppermute | solution.py:390
  45.5 2.3 %collective-permute-done.1.refs_3_ = f32[328,128]{1,0:T(8,128)S(1)} collective-permute-done((f32[328,128]{1,0:T(8,128)S(1)}, f32[328,128]{1,0:T(8,128)S(1)}, u32[]{:S(2)}, u32[]{:S(2)}) %collective-permute-start.1) | collective-permute-done | bytes 167968 | tf_op jit(solution)/shard_map/ppermute | solution.py:391
  47.8 0.0 collective-permute-done.refs_2_
  47.8 0.7 shard_map.77
  48.5 3.9 %collective-permute-start.3 = (f32[328,128]{1,0:T(8,128)S(1)}, f32[328,128]{1,0:T(8,128)S(1)}, u32[]{:S(2)}, u32[]{:S(2)}) collective-permute-start(f32[328,128]{1,0:T(8,128)S(1)} %get-tuple-element.30.refs_10_), channel_id=1, source_target_pairs={{1,2},{2,1},{3,4},{4,3},{5,6},{6,5},{7,8},{8,7},{9,10},{10,9},{11,... | collective-permute-start | bytes 503816 | tf_op jit(solution)/shard_map/ppermute | solution.py:391
  52.4 1.9 %collective-permute-start.2 = (f32[328,128]{1,0:T(8,128)S(1)}, f32[328,128]{1,0:T(8,128)S(1)}, u32[]{:S(2)}, u32[]{:S(2)}) collective-permute-start(f32[328,128]{1,0:T(8,128)S(1)} %get-tuple-element.30.refs_10_), channel_id=1, source_target_pairs={{0,1},{1,0},{2,3},{3,2},{4,5},{5,4},{6,7},{7,6},{8,9},{9,8},{10,11... | collective-permute-start | bytes 503816 | tf_op jit(solution)/shard_map/ppermute | solution.py:390
  54.3 10.3 %all_to_all.16.refs_9_ = f32[16,1,128]{2,1,0:T(1,128)S(1)} all-to-all(f32[16,1,128]{2,1,0:T(1,128)S(1)} %get-tuple-element.29), channel_id=1, replica_groups=mesh['harm'=32,'slab'=16] {'slab'}, dimensions={0} | all-to-all | bytes 16384 | tf_op jit(solution)/shard_map/all_to_all | solution.py:381
  64.6 0.0 collective-permute-done.3.refs_12_
  64.6 0.0 collective-permute-done.2.refs_11_
  64.6 0.8 shard_map.78
  65.4 3.6 %collective-permute-start.5 = (f32[328,128]{1,0:T(8,128)S(1)}, f32[328,128]{1,0:T(8,128)S(1)}, u32[]{:S(2)}, u32[]{:S(2)}) collective-permute-start(f32[328,128]{1,0:T(8,128)S(1)} %get-tuple-element.32.refs_1_), channel_id=1, source_target_pairs={{1,2},{2,1},{3,4},{4,3},{5,6},{6,5},{7,8},{8,7},{9,10},{10,9},{11,... | collective-permute-start | bytes 503816 | tf_op jit(solution)/shard_map/ppermute | solution.py:391
  69.1 1.9 %collective-permute-start.4 = (f32[328,128]{1,0:T(8,128)S(1)}, f32[328,128]{1,0:T(8,128)S(1)}, u32[]{:S(2)}, u32[]{:S(2)}) collective-permute-start(f32[328,128]{1,0:T(8,128)S(1)} %get-tuple-element.32.refs_1_), channel_id=1, source_target_pairs={{0,1},{1,0},{2,3},{3,2},{4,5},{5,4},{6,7},{7,6},{8,9},{9,8},{10,11... | collective-permute-start | bytes 503816 | tf_op jit(solution)/shard_map/ppermute | solution.py:390
  71.0 2.9 %collective-permute-done.5.refs_3_ = f32[328,128]{1,0:T(8,128)S(1)} collective-permute-done((f32[328,128]{1,0:T(8,128)S(1)}, f32[328,128]{1,0:T(8,128)S(1)}, u32[]{:S(2)}, u32[]{:S(2)}) %collective-permute-start.5) | collective-permute-done | bytes 167968 | tf_op jit(solution)/shard_map/ppermute | solution.py:391
  73.9 0.0 collective-permute-done.4.refs_2_
  73.9 0.7 shard_map.79
  74.6 4.5 %collective-permute-start.7 = (f32[328,128]{1,0:T(8,128)S(1)}, f32[328,128]{1,0:T(8,128)S(1)}, u32[]{:S(2)}, u32[]{:S(2)}) collective-permute-start(f32[328,128]{1,0:T(8,128)S(1)} %get-tuple-element.34.refs_1_), channel_id=1, source_target_pairs={{1,2},{2,1},{3,4},{4,3},{5,6},{6,5},{7,8},{8,7},{9,10},{10,9},{11,... | collective-permute-start | bytes 503816 | tf_op jit(solution)/shard_map/ppermute | solution.py:391
  79.2 1.9 %collective-permute-start.6 = (f32[328,128]{1,0:T(8,128)S(1)}, f32[328,128]{1,0:T(8,128)S(1)}, u32[]{:S(2)}, u32[]{:S(2)}) collective-permute-start(f32[328,128]{1,0:T(8,128)S(1)} %get-tuple-element.34.refs_1_), channel_id=1, source_target_pairs={{0,1},{1,0},{2,3},{3,2},{4,5},{5,4},{6,7},{7,6},{8,9},{9,8},{10,11... | collective-permute-start | bytes 503816 | tf_op jit(solution)/shard_map/ppermute | solution.py:390
  81.1 1.5 %collective-permute-done.7.refs_3_ = f32[328,128]{1,0:T(8,128)S(1)} collective-permute-done((f32[328,128]{1,0:T(8,128)S(1)}, f32[328,128]{1,0:T(8,128)S(1)}, u32[]{:S(2)}, u32[]{:S(2)}) %collective-permute-start.7) | collective-permute-done | bytes 167968 | tf_op jit(solution)/shard_map/ppermute | solution.py:391
  82.6 0.0 collective-permute-done.6.refs_2_
  82.6 1.0 shard_map.80
  83.6 25.3 %all_to_all.17.arrived_ref = f32[32,4,512]{2,1,0:T(4,128)S(1)} all-to-all(f32[32,4,512]{2,1,0:T(4,128)S(1)} %shard_map.80), channel_id=1, replica_groups=mesh['harm'=32,'slab'=16] {'harm'}, dimensions={0} | all-to-all | bytes 524288 | tf_op jit(solution)/shard_map/all_to_all | solution.py:418
  108.9 0.9 restore.1
Async XLA Ops:
  37.3 10.5 %collective-permute-start.1 = (f32[328,128]{1,0:T(8,128)S(1)}, f32[328,128]{1,0:T(8,128)S(1)}, u32[]{:S(2)}, u32[]{:S(2)}) collective-permute-start(f32[328,128]{1,0:T(8,128)S(1)} %get-tuple-element.21.refs_1_.refs_10_), channel_id=1, source_target_pairs={{1,2},{2,1},{3,4},{4,3},{5,6},{6,5},{7,8},{8,7},{9,10},{10,9},{11,... | collective-permute-start | bytes 503816 | tf_op jit(solution)/shard_map/ppermute | solution.py:391
  43.5 4.2 %collective-permute-start = (f32[328,128]{1,0:T(8,128)S(1)}, f32[328,128]{1,0:T(8,128)S(1)}, u32[]{:S(2)}, u32[]{:S(2)}) collective-permute-start(f32[328,128]{1,0:T(8,128)S(1)} %get-tuple-element.21.refs_1_.refs_10_), channel_id=1, source_target_pairs={{0,1},{1,0},{2,3},{3,2},{4,5},{5,4},{6,7},{7,6},{8,9},{9,8},{10,11... | collective-permute-start | bytes 503816 | tf_op jit(solution)/shard_map/ppermute | solution.py:390
  48.5 16.1 %collective-permute-start.3 = (f32[328,128]{1,0:T(8,128)S(1)}, f32[328,128]{1,0:T(8,128)S(1)}, u32[]{:S(2)}, u32[]{:S(2)}) collective-permute-start(f32[328,128]{1,0:T(8,128)S(1)} %get-tuple-element.30.refs_10_), channel_id=1, source_target_pairs={{1,2},{2,1},{3,4},{4,3},{5,6},{6,5},{7,8},{8,7},{9,10},{10,9},{11,... | collective-permute-start | bytes 503816 | tf_op jit(solution)/shard_map/ppermute | solution.py:391
  52.4 12.2 %collective-permute-start.2 = (f32[328,128]{1,0:T(8,128)S(1)}, f32[328,128]{1,0:T(8,128)S(1)}, u32[]{:S(2)}, u32[]{:S(2)}) collective-permute-start(f32[328,128]{1,0:T(8,128)S(1)} %get-tuple-element.30.refs_10_), channel_id=1, source_target_pairs={{0,1},{1,0},{2,3},{3,2},{4,5},{5,4},{6,7},{7,6},{8,9},{9,8},{10,11... | collective-permute-start | bytes 503816 | tf_op jit(solution)/shard_map/ppermute | solution.py:390
  65.4 8.5 %collective-permute-start.5 = (f32[328,128]{1,0:T(8,128)S(1)}, f32[328,128]{1,0:T(8,128)S(1)}, u32[]{:S(2)}, u32[]{:S(2)}) collective-permute-start(f32[328,128]{1,0:T(8,128)S(1)} %get-tuple-element.32.refs_1_), channel_id=1, source_target_pairs={{1,2},{2,1},{3,4},{4,3},{5,6},{6,5},{7,8},{8,7},{9,10},{10,9},{11,... | collective-permute-start | bytes 503816 | tf_op jit(solution)/shard_map/ppermute | solution.py:391
  69.1 4.8 %collective-permute-start.4 = (f32[328,128]{1,0:T(8,128)S(1)}, f32[328,128]{1,0:T(8,128)S(1)}, u32[]{:S(2)}, u32[]{:S(2)}) collective-permute-start(f32[328,128]{1,0:T(8,128)S(1)} %get-tuple-element.32.refs_1_), channel_id=1, source_target_pairs={{0,1},{1,0},{2,3},{3,2},{4,5},{5,4},{6,7},{7,6},{8,9},{9,8},{10,11... | collective-permute-start | bytes 503816 | tf_op jit(solution)/shard_map/ppermute | solution.py:390
  74.6 7.9 %collective-permute-start.7 = (f32[328,128]{1,0:T(8,128)S(1)}, f32[328,128]{1,0:T(8,128)S(1)}, u32[]{:S(2)}, u32[]{:S(2)}) collective-permute-start(f32[328,128]{1,0:T(8,128)S(1)} %get-tuple-element.34.refs_1_), channel_id=1, source_target_pairs={{1,2},{2,1},{3,4},{4,3},{5,6},{6,5},{7,8},{8,7},{9,10},{10,9},{11,... | collective-permute-start | bytes 503816 | tf_op jit(solution)/shard_map/ppermute | solution.py:391
  79.2 3.4 %collective-permute-start.6 = (f32[328,128]{1,0:T(8,128)S(1)}, f32[328,128]{1,0:T(8,128)S(1)}, u32[]{:S(2)}, u32[]{:S(2)}) collective-permute-start(f32[328,128]{1,0:T(8,128)S(1)} %get-tuple-element.34.refs_1_), channel_id=1, source_target_pairs={{0,1},{1,0},{2,3},{3,2},{4,5},{5,4},{6,7},{7,6},{8,9},{9,8},{10,11... | collective-permute-start | bytes 503816 | tf_op jit(solution)/shard_map/ppermute | solution.py:390
where the time goes:
time: 112 us; the launch traced here: 110 us
  blocking collectives  70.2 us (63%)
  starting transfers between devices  26 us (23%)
  waiting for transfers between devices  6.63 us (6%)
  Pallas kernels  5.59 us (5%)
  between operations  1.4 us (1%)
    all_to_all x1, blocking collectives, shards(): arrived = lax.all_to_all(sends, 'harm', 0, 0, tiled=True)  34.5 us
    all_to_all x1, blocking collectives, shards(): back = lax.all_to_all(result, 'harm', 0, 0, tiled=True)  25.3 us
    ppermute x4, starting transfers between devices, beside(): chip = lax.ppermute(state, 'slab', chip_pairs)  18.4 us
    all_to_all x1, blocking collectives, shards(): speeds = lax.all_to_all(speed, 'slab', 0, 0, tiled=True)  10.3 us
    ppermute x4, starting transfers between devices, beside(): core = lax.ppermute(state, 'slab', core_pairs)  7.68 us
    ppermute x4, waiting for transfers between devices, beside(): chip = lax.ppermute(state, 'slab', chip_pairs)  6.62 us
    pallas_call x4, Pallas kernels, section(): pl.pallas_call(functools.partial(section_kernel, stage=stage, cell_count=...  3.24 us
  transfers between devices with their start and end apart: 8, of which 3 were waited for; matrix products, arithmetic and copies ran while one was open for 0% of the time, Pallas kernels for 0%

commit v1 on v0

--- a/solution.py
+++ b/solution.py
@@ -24,6 +24,7 @@
 H_ROWS = 2 * VARS * CELLS * C1
 M_ROWS = VARS * CELLS * C1
 W_ROWS = CELLS * C1
+F_END = H_ROWS + M_ROWS + 4 * CELLS * C1
 
 
 def h_row(part, var, cell):
@@ -110,17 +111,7 @@
     omega_out[...] = turned[H_ROWS : H_ROWS + 8, :]
 
 
-def section_kernel(*refs, stage, cell_count):
-    last = stage == len(SECTION_RATES) - 1
-    parity_ref, own_ref, core_ref, chip_ref, *refs = refs
-    mean_ref, omega_ref, wall_ref, jac_ref, radius_ref, *refs = refs
-    if stage == 0:
-        outs = refs
-    elif stage == 1:
-        speed_ref, own_res, core_res, chip_res, mean_res, *outs = refs
-        h0_ref, m0_ref = own_ref, mean_ref
-    else:
-        speed_ref, h0_ref, m0_ref, *outs = refs
+def tile_tools(jac_ref):
     lane = lax.broadcasted_iota(jnp.int32, (C1, LANES), 1)
     even = (lane // 2) % 2 == 0
 
@@ -134,8 +125,10 @@
         swapped = jnp.where(even, pltpu.roll(tile, LANES - 2, 1), pltpu.roll(tile, 2, 1))
         return jnp.where(even, swapped, up(swapped)), jnp.where(even, down(swapped), swapped)
 
-    def splat(ref, row):
-        return jnp.broadcast_to(ref[row : row + 1, :], (C1, LANES))
+    def cross_parts(center):
+        above, below = beside(center)
+        fourth = (up(center) + down(center)) - 4.0 * (above + below) + 12.0 * center
+        return (above - below) * 0.5, fourth
 
     def apply_matrix(base, tiles):
         out = []
@@ -146,136 +139,177 @@
             out.append(total)
         return out
 
+    return lane, beside, cross_parts, apply_matrix
+
+
+def splat(ref, row):
+    return jnp.broadcast_to(ref[row : row + 1, :], (C1, LANES))
+
+
+def time_step_of(speed_ref, cell_count):
+    speed_total = jnp.sum(speed_ref[...], axis=0)
+    time_step = COURANT / (1.0 + jnp.sqrt(speed_total / cell_count))
+    return jnp.broadcast_to(time_step, (C1, LANES))
+
+
+def load(block, row, first, count=C1):
+    base, residual = block
+    value = base[row : row + count, :]
+    if residual is not None:
+        value = value + first[:count] * residual[row : row + count, :]
+    return value
+
+
+def stress(left, right, index):
+    a, b = STRESS_PAIRS[index]
+    return 0.5 * (left[a] * left[b] + right[a] * right[b])
+
+
+def own_terms(own, mean_block, first, omega_ref, wall_ref, jac_ref, radius_ref):
+    _, beside, cross_parts, apply_matrix = tile_tools(jac_ref)
     omega = splat(omega_ref, 0)
-    if stage:
-        speed_total = jnp.sum(speed_ref[...], axis=0)
-        time_step = COURANT / (1.0 + jnp.sqrt(speed_total / cell_count))
-        time_step = jnp.broadcast_to(time_step, (C1, LANES))
+    inv_radius = 1.0 / splat(radius_ref, 0)
+    rows = {}
+    for cell in range(CELLS):
+        wall = WALL_RATE * wall_ref[cell * C1 : (cell + 1) * C1, :]
+        harm = [
+            [load(own, h_row(part, var, cell), first) for var in range(VARS)] for part in range(2)
+        ]
+        for part in range(2):
+            diffs, fourths = zip(*[cross_parts(tile) for tile in harm[part]])
+            flux = apply_matrix(VARS * VARS, diffs)
+            for var in range(VARS):
+                turned = omega * harm[1 - part][var]
+                if part:
+                    turned = -turned
+                rows[h_row(part, var, cell)] = (
+                    turned - flux[var] - EPS_FOURTH * fourths[var] - wall * harm[part][var]
+                )
+        mean = [load(mean_block, m_row(var, cell), first) for var in range(VARS)]
+        diffs, fourths = zip(*[cross_parts(tile) for tile in mean])
+        flux = apply_matrix(VARS * VARS, diffs)
+        for var in range(VARS):
+            rows[H_ROWS + m_row(var, cell)] = -flux[var] - EPS_FOURTH * fourths[var]
+
+        def grad_y(tile):
+            above, below = beside(tile)
+            return (above - below) * 0.5
+
+        s = [stress(*harm, index) for index in range(len(STRESS_PAIRS))]
+        terms = [
+            -grad_y(s[1]),
+            -grad_y(s[3]) - 2.0 * s[4] * inv_radius,
+            -grad_y(s[4]) + (s[3] - s[5]) * inv_radius,
+            -grad_y(s[7]) - s[8] * inv_radius,
+        ]
+        for index, term in enumerate(terms):
+            rows[f_row(index, cell)] = term
+    return rows
+
+
+def f_row(index, cell):
+    return H_ROWS + M_ROWS + (index * CELLS + cell) * C1
+
+
+def own_kernel(*refs, stage, cell_count):
+    own_ref, mean_ref, omega_ref, wall_ref, jac_ref, radius_ref, *refs, out_ref = refs
+    own, mean_block, first = (own_ref, None), (mean_ref, None), None
+    if stage == 1:
+        speed_ref, own_res, mean_res = refs
+        first = SECTION_RATES[0] * time_step_of(speed_ref, cell_count)
+        own, mean_block = (own_ref, own_res), (mean_ref, mean_res)
+    rows = own_terms(own, mean_block, first, omega_ref, wall_ref, jac_ref, radius_ref)
+    for row, tile in rows.items():
+        out_ref[row : row + C1, :] = tile
+
+
+def section_kernel(*refs, stage, cell_count):
+    last = stage == len(SECTION_RATES) - 1
+    parity_ref, own_ref, core_ref, chip_ref, mean_ref, *refs = refs
+    own, core, chip = (own_ref, None), (core_ref, None), (chip_ref, None)
+    mean_block, first = (mean_ref, None), None
+    if stage == 0:
+        omega_ref, wall_ref, jac_ref, radius_ref, *outs = refs
+        near = own_terms(own, mean_block, first, omega_ref, wall_ref, jac_ref, radius_ref)
+    else:
+        jac_ref, near_ref, speed_ref, *refs = refs
+        time_step = time_step_of(speed_ref, cell_count)
         step = SECTION_RATES[stage] * time_step
-    own, core, chip = (own_ref, None), (core_ref, None), (chip_ref, None)
-    mean_block = (mean_ref, None)
     if stage == 1:
         first = SECTION_RATES[0] * time_step
+        own_res, core_res, chip_res, mean_res, *outs = refs
         own, core, chip = (own_ref, own_res), (core_ref, core_res), (chip_ref, chip_res)
         mean_block = (mean_ref, mean_res)
-
-    def load(block, row, count=C1):
-        base, residual = block
-        value = base[row : row + count, :]
-        if residual is not None:
-            value = value + first[:count] * residual[row : row + count, :]
-        return value
-
+        h0_ref, m0_ref = own_ref, mean_ref
+    elif stage:
+        h0_ref, m0_ref, *outs = refs
+    lane, _, _, apply_matrix = tile_tools(jac_ref)
     on_first = parity_ref[0] == 0
 
+    def near_term(row):
+        return near_ref[row : row + C1, :] if stage else near[row]
+
     def sides(row, count=C1):
-        paired, other = load(core, row, count), load(chip, row, count)
+        paired, other = load(core, row, first, count), load(chip, row, first, count)
         return jnp.where(on_first, other, paired), jnp.where(on_first, paired, other)
 
     def column(part, var):
         rows = [h_row(part, var, cell) for cell in range(CELLS)]
         left, right = zip(*[sides(row) for row in rows])
-        return [*left, *[load(own, row) for row in rows], *right]
-
-    inv_radius = 1.0 / splat(radius_ref, 0)
+        return [*left, *[load(own, row, first) for row in rows], *right]
 
     harm = [[column(part, var) for var in range(VARS)] for part in range(2)]
     left_mean, right_mean = [unpack_mean(packed) for packed in sides(H_ROWS, 8)]
     mean = []
     for var in range(VARS):
-        own_mean = [load(mean_block, m_row(var, cell)) for cell in range(CELLS)]
+        own_mean = [load(mean_block, m_row(var, cell), first) for cell in range(CELLS)]
         mean.append(
             left_mean[CELLS * var : CELLS * (var + 1)]
             + own_mean
             + right_mean[CELLS * var : CELLS * (var + 1)]
         )
 
-    def smooth_parts(cells, at):
-        center = cells[at]
-        above, below = beside(center)
-        diff_y = (above - below) * 0.5
-        fourth = (
-            (cells[at + 2] + cells[at - 2])
-            + (up(center) + down(center))
-            - 4.0 * ((cells[at + 1] + cells[at - 1]) + (above + below))
-            + 12.0 * center
-        )
-        return diff_y, fourth
-
-    harm_new = {}
-    for cell in range(CELLS):
-        at = 2 + cell
-        wall = WALL_RATE * wall_ref[cell * C1 : (cell + 1) * C1, :]
-        for part in range(2):
-            diffs_x, diffs_y, fourths = [], [], []
-            for var in range(VARS):
-                cells = harm[part][var]
-                diffs_x.append(
-                    (mean[1][at + 1] * cells[at + 1] - mean[1][at - 1] * cells[at - 1]) * 0.5
-                )
-                diff_y, fourth = smooth_parts(cells, at)
-                diffs_y.append(diff_y)
-                fourths.append(fourth)
-            flux_x = apply_matrix(0, diffs_x)
-            flux_y = apply_matrix(VARS * VARS, diffs_y)
-            for var in range(VARS):
-                turned = omega * harm[1 - part][var][at]
-                if part:
-                    turned = -turned
-                res = (
-                    turned
-                    - flux_x[var]
-                    - flux_y[var]
-                    - EPS_FOURTH * fourths[var]
-                    - wall * harm[part][var][at]
-                )
-                row = h_row(part, var, cell)
-                if stage:
-                    res = h0_ref[row : row + C1, :] + step * res
-                harm_new[part, var, cell] = res
-
-    def stress(index, at):
-        a, b = STRESS_PAIRS[index]
-        return 0.5 * (harm[0][a][at] * harm[0][b][at] + harm[1][a][at] * harm[1][b][at])
+    def axial_fourth(cells, at):
+        return (cells[at + 2] + cells[at - 2]) - 4.0 * (cells[at + 1] + cells[at - 1])
 
     def total(tile):
         for shift in (4, 8, 16, 32, 64):
             tile = tile + pltpu.roll(tile, shift, 1)
         return jnp.take_along_axis(tile, lane % 4, axis=1)
 
-    mean_new = {}
+    harm_new, mean_new = {}, {}
     for cell in range(CELLS):
         at = 2 + cell
+        for part in range(2):
+            diffs = [
+                (mean[1][at + 1] * cells[at + 1] - mean[1][at - 1] * cells[at - 1]) * 0.5
+                for cells in harm[part]
+            ]
+            flux = apply_matrix(0, diffs)
+            for var in range(VARS):
+                row = h_row(part, var, cell)
+                res = near_term(row) - flux[var] - EPS_FOURTH * axial_fourth(harm[part][var], at)
+                if stage:
+                    res = h0_ref[row : row + C1, :] + step * res
+                harm_new[part, var, cell] = res
 
         def grad_x(index):
-            return (stress(index, at + 1) - stress(index, at - 1)) * 0.5
-
-        def grad_y(tile):
-            above, below = beside(tile)
+            above, below = [
+                stress(*[[cells[x] for cells in harm[part]] for part in range(2)], index)
+                for x in (at + 1, at - 1)
+            ]
             return (above - below) * 0.5
 
-        s3, s4 = stress(3, at), stress(4, at)
         terms = [
-            None,
-            total(-grad_x(0) - grad_y(stress(1, at))),
-            total(-grad_x(1) - grad_y(s3) - 2.0 * s4 * inv_radius),
-            total(-grad_x(2) - grad_y(s4) + (s3 - stress(5, at)) * inv_radius),
-            total(-grad_x(6) - grad_y(stress(7, at)) - stress(8, at) * inv_radius),
+            total(near_term(f_row(i, cell)) - grad_x(index))
+            for i, index in enumerate((0, 1, 2, 6))
         ]
-        diffs_x, diffs_y, fourths = [], [], []
+        flux = apply_matrix(0, [(cells[at + 1] - cells[at - 1]) * 0.5 for cells in mean])
         for var in range(VARS):
-            cells = mean[var]
-            diffs_x.append((cells[at + 1] - cells[at - 1]) * 0.5)
-            diff_y, fourth = smooth_parts(cells, at)
-            diffs_y.append(diff_y)
-            fourths.append(fourth)
-        flux_x = apply_matrix(0, diffs_x)
-        flux_y = apply_matrix(VARS * VARS, diffs_y)
-        for var in range(VARS):
-            res = -flux_x[var] - flux_y[var] - EPS_FOURTH * fourths[var]
+            row = m_row(var, cell)
+            res = near_term(H_ROWS + row) - flux[var] - EPS_FOURTH * axial_fourth(mean[var], at)
             if var:
-                res = res + terms[var]
-            row = m_row(var, cell)
+                res = res + terms[var - 1]
             if stage:
                 res = m0_ref[row : row + C1, :] + step * res
             mean_new[var, cell] = res
@@ -285,7 +319,7 @@
         target, offset = rows_ref, H_ROWS
     else:
         state_out, mean_out = outs
-        target, offset = state_out, None
+        target = state_out
     for (part, var, cell), tile in harm_new.items():
         row = h_row(part, var, cell)
         target[row : row + C1, :] = tile
@@ -406,15 +440,31 @@
             scratch_shapes=scratch,
         )(parity, *held(*operands))
 
+    def own_part(stage, *operands):
+        return pl.pallas_call(
+            functools.partial(own_kernel, stage=stage, cell_count=cell_count),
+            out_shape=[kept(F_END, LANES)],
+            in_specs=[VMEM] * len(operands),
+            out_specs=[VMEM],
+        )(*held(*operands))
+
     parity = (lax.axis_index("slab") % 2).astype(jnp.int32).reshape(1)
     fixed = (omega, wall, jac, radius)
-    start_blocks = beside(start)
-    residual, mean_residual = section(0, *start_blocks, mean_start, *fixed)
+    blocks = beside(start)
+    residual, mean_residual = section(0, *blocks, mean_start, *fixed)
+    residual_blocks = beside(residual)
+    (near,) = own_part(1, start, mean_start, *fixed, speeds, residual, mean_residual)
     state, mean_now = section(
-        1, *start_blocks, mean_start, *fixed, speeds, *beside(residual), mean_residual
-    )
-    state, mean_now = section(2, *beside(state), mean_now, *fixed, speeds, start, mean_start)
-    result = section(3, *beside(state), mean_now, *fixed, speeds, start, mean_start)
+        1, *blocks, mean_start, jac, near, speeds, *residual_blocks, mean_residual
+    )
+    blocks = beside(state)
+    (near,) = own_part(2, state, mean_now, *fixed)
+    state, mean_now = section(
+        2, *blocks, mean_now, jac, near, speeds, start, mean_start
+    )
+    blocks = beside(state)
+    (near,) = own_part(3, state, mean_now, *fixed)
+    result = section(3, *blocks, mean_now, jac, near, speeds, start, mean_start)
     back = lax.all_to_all(result, "harm", 0, 0, tiled=True)
     return pl.pallas_call(
         restore_kernel,

time: 112 us -> 111 us (level)
    pallas_call x0 -> x3, Pallas kernels: none -> 1.15 us  [own_part(): pl.pallas_call(functools.partial(own_kernel, stage=stage, cell_count=cell...]
  transfers between devices with their start and end apart: 8 -> 8, of which waited for: 3 -> 3; matrix products, arithmetic and copies ran while one was open for 0% -> 0% of each run, Pallas kernels for 0% -> 1%
where the time goes in v1:
time: 111 us; the launch traced here: 109 us
  blocking collectives  70.2 us (63%)
  starting transfers between devices  26 us (23%)
  Pallas kernels  5.92 us (5%)
  waiting for transfers between devices  5.88 us (5%)
  between operations  1.43 us (1%)
    all_to_all x1, blocking collectives, shards(): arrived = lax.all_to_all(sends, 'harm', 0, 0, tiled=True)  34.5 us
    all_to_all x1, blocking collectives, shards(): back = lax.all_to_all(result, 'harm', 0, 0, tiled=True)  25.3 us
    ppermute x4, starting transfers between devices, beside(): chip = lax.ppermute(state, 'slab', chip_pairs)  18.4 us
    all_to_all x1, blocking collectives, shards(): speeds = lax.all_to_all(speed, 'slab', 0, 0, tiled=True)  10.3 us
    ppermute x4, starting transfers between devices, beside(): core = lax.ppermute(state, 'slab', core_pairs)  7.68 us
    ppermute x4, waiting for transfers between devices, beside(): chip = lax.ppermute(state, 'slab', chip_pairs)  5.87 us
    pallas_call x4, Pallas kernels, section(): pl.pallas_call(functools.partial(section_kernel, stage=stage, cell_count=...  2.42 us
  transfers between devices with their start and end apart: 8, of which 3 were waited for; matrix products, arithmetic and copies ran while one was open for 0% of the time, Pallas kernels for 1%

profile of v1, /device:TPU:7, one launch (start us, length us, event | category | flops | bytes accessed | tf_op | source)
XLA Modules:
  0.0 109.4 jit_solution(228982127572374951)
XLA Ops:
  1.3 1.3 %open.1 = (f32[32,4,384]{2,1,0:T(4,128)S(1)}, f32[160,128]{1,0:T(8,128)S(1)}, f32[32,128]{1,0:T(8,128)S(1)}, f32[8,128]{1,0:T(8,128)S(1)}, f32[16,1,128]{2,1,0:T...) custom-call(f32[1,2,5,2,2048]{4,3,2,1,0:T(2,128)} %harm_ref.1, f32[5,2,2048]{2,1,0:T(2,128)} %mean_ref.1, ...), custom_call_target="tpu_custom_call" | custom-call | tf_op jit(solution)/shard_map/open/pallas_call | solution.py:385
  2.6 34.5 %all_to_all.15.arrived_ref = f32[32,4,384]{2,1,0:T(4,128)S(1)} all-to-all(f32[32,4,384]{2,1,0:T(4,128)S(1)} %get-tuple-element.19), channel_id=1, replica_groups=mesh['harm'=32,'slab'=16] {'harm'}, dimensions={0} | all-to-all | bytes 393216 | tf_op jit(solution)/shard_map/all_to_all | solution.py:404
  37.1 0.1 unpack.1
  37.3 6.3 %collective-permute-start.1 = (f32[328,128]{1,0:T(8,128)S(1)}, f32[328,128]{1,0:T(8,128)S(1)}, u32[]{:S(2)}, u32[]{:S(2)}) collective-permute-start(f32[328,128]{1,0:T(8,128)S(1)} %get-tuple-element.21.refs_1_.refs_0_.refs_8_), channel_id=1, source_target_pairs={{1,2},{2,1},{3,4},{4,3},{5,6},{6,5},{7,8},{8,7},{9,10},{10,9},{11,... | collective-permute-start | bytes 503816 | tf_op jit(solution)/shard_map/ppermute | solution.py:425
  43.5 1.9 %collective-permute-start = (f32[328,128]{1,0:T(8,128)S(1)}, f32[328,128]{1,0:T(8,128)S(1)}, u32[]{:S(2)}, u32[]{:S(2)}) collective-permute-start(f32[328,128]{1,0:T(8,128)S(1)} %get-tuple-element.21.refs_1_.refs_0_.refs_8_), channel_id=1, source_target_pairs={{0,1},{1,0},{2,3},{3,2},{4,5},{5,4},{6,7},{7,6},{8,9},{9,8},{10,11... | collective-permute-start | bytes 503816 | tf_op jit(solution)/shard_map/ppermute | solution.py:424
  45.5 2.3 %collective-permute-done.1.refs_3_ = f32[328,128]{1,0:T(8,128)S(1)} collective-permute-done((f32[328,128]{1,0:T(8,128)S(1)}, f32[328,128]{1,0:T(8,128)S(1)}, u32[]{:S(2)}, u32[]{:S(2)}) %collective-permute-start.1) | collective-permute-done | bytes 167968 | tf_op jit(solution)/shard_map/ppermute | solution.py:425
  47.8 0.0 collective-permute-done.refs_2_
  47.8 0.7 shard_map.77
  48.5 3.9 %collective-permute-start.3 = (f32[328,128]{1,0:T(8,128)S(1)}, f32[328,128]{1,0:T(8,128)S(1)}, u32[]{:S(2)}, u32[]{:S(2)}) collective-permute-start(f32[328,128]{1,0:T(8,128)S(1)} %get-tuple-element.30.refs_7_.refs_8_), channel_id=1, source_target_pairs={{1,2},{2,1},{3,4},{4,3},{5,6},{6,5},{7,8},{8,7},{9,10},{10,9},{11,... | collective-permute-start | bytes 503816 | tf_op jit(solution)/shard_map/ppermute | solution.py:425
  52.4 1.9 %collective-permute-start.2 = (f32[328,128]{1,0:T(8,128)S(1)}, f32[328,128]{1,0:T(8,128)S(1)}, u32[]{:S(2)}, u32[]{:S(2)}) collective-permute-start(f32[328,128]{1,0:T(8,128)S(1)} %get-tuple-element.30.refs_7_.refs_8_), channel_id=1, source_target_pairs={{0,1},{1,0},{2,3},{3,2},{4,5},{5,4},{6,7},{7,6},{8,9},{9,8},{10,11... | collective-permute-start | bytes 503816 | tf_op jit(solution)/shard_map/ppermute | solution.py:424
  54.3 10.3 %all_to_all.16.refs_6_.refs_7_ = f32[16,1,128]{2,1,0:T(1,128)S(1)} all-to-all(f32[16,1,128]{2,1,0:T(1,128)S(1)} %get-tuple-element.29), channel_id=1, replica_groups=mesh['harm'=32,'slab'=16] {'slab'}, dimensions={0} | all-to-all | bytes 16384 | tf_op jit(solution)/shard_map/all_to_all | solution.py:415
  64.6 0.4 shard_map.78.refs_6_
  65.1 0.0 collective-permute-done.3.refs_10_
  65.1 0.0 collective-permute-done.2.refs_9_
  65.1 0.6 shard_map.79
  65.7 3.6 %collective-permute-start.5 = (f32[328,128]{1,0:T(8,128)S(1)}, f32[328,128]{1,0:T(8,128)S(1)}, u32[]{:S(2)}, u32[]{:S(2)}) collective-permute-start(f32[328,128]{1,0:T(8,128)S(1)} %get-tuple-element.32.refs_0_.refs_1_), channel_id=1, source_target_pairs={{1,2},{2,1},{3,4},{4,3},{5,6},{6,5},{7,8},{8,7},{9,10},{10,9},{11,... | collective-permute-start | bytes 503816 | tf_op jit(solution)/shard_map/ppermute | solution.py:425
  69.3 1.9 %collective-permute-start.4 = (f32[328,128]{1,0:T(8,128)S(1)}, f32[328,128]{1,0:T(8,128)S(1)}, u32[]{:S(2)}, u32[]{:S(2)}) collective-permute-start(f32[328,128]{1,0:T(8,128)S(1)} %get-tuple-element.32.refs_0_.refs_1_), channel_id=1, source_target_pairs={{0,1},{1,0},{2,3},{3,2},{4,5},{5,4},{6,7},{7,6},{8,9},{9,8},{10,11... | collective-permute-start | bytes 503816 | tf_op jit(solution)/shard_map/ppermute | solution.py:424
  71.2 0.4 shard_map.80.refs_6_
  71.6 2.5 %collective-permute-done.5.refs_3_ = f32[328,128]{1,0:T(8,128)S(1)} collective-permute-done((f32[328,128]{1,0:T(8,128)S(1)}, f32[328,128]{1,0:T(8,128)S(1)}, u32[]{:S(2)}, u32[]{:S(2)}) %collective-permute-start.5) | collective-permute-done | bytes 167968 | tf_op jit(solution)/shard_map/ppermute | solution.py:425
  74.1 0.0 collective-permute-done.4.refs_2_
  74.1 0.5 shard_map.81
  74.6 4.5 %collective-permute-start.7 = (f32[328,128]{1,0:T(8,128)S(1)}, f32[328,128]{1,0:T(8,128)S(1)}, u32[]{:S(2)}, u32[]{:S(2)}) collective-permute-start(f32[328,128]{1,0:T(8,128)S(1)} %get-tuple-element.34.refs_0_.refs_1_), channel_id=1, source_target_pairs={{1,2},{2,1},{3,4},{4,3},{5,6},{6,5},{7,8},{8,7},{9,10},{10,9},{11,... | collective-permute-start | bytes 503816 | tf_op jit(solution)/shard_map/ppermute | solution.py:425
  79.2 1.9 %collective-permute-start.6 = (f32[328,128]{1,0:T(8,128)S(1)}, f32[328,128]{1,0:T(8,128)S(1)}, u32[]{:S(2)}, u32[]{:S(2)}) collective-permute-start(f32[328,128]{1,0:T(8,128)S(1)} %get-tuple-element.34.refs_0_.refs_1_), channel_id=1, source_target_pairs={{0,1},{1,0},{2,3},{3,2},{4,5},{5,4},{6,7},{7,6},{8,9},{9,8},{10,11... | collective-permute-start | bytes 503816 | tf_op jit(solution)/shard_map/ppermute | solution.py:424
  81.1 0.4 shard_map.82.refs_6_
  81.5 1.1 collective-permute-done.7.refs_3_
  82.5 0.0 collective-permute-done.6.refs_2_
  82.6 0.6 shard_map.83
  83.2 25.3 %all_to_all.17.arrived_ref = f32[32,4,512]{2,1,0:T(4,128)S(1)} all-to-all(f32[32,4,512]{2,1,0:T(4,128)S(1)} %shard_map.83), channel_id=1, replica_groups=mesh['harm'=32,'slab'=16] {'harm'}, dimensions={0} | all-to-all | bytes 524288 | tf_op jit(solution)/shard_map/all_to_all | solution.py:468
  108.5 0.9 restore.1
Async XLA Ops:
  37.3 10.5 %collective-permute-start.1 = (f32[328,128]{1,0:T(8,128)S(1)}, f32[328,128]{1,0:T(8,128)S(1)}, u32[]{:S(2)}, u32[]{:S(2)}) collective-permute-start(f32[328,128]{1,0:T(8,128)S(1)} %get-tuple-element.21.refs_1_.refs_0_.refs_8_), channel_id=1, source_target_pairs={{1,2},{2,1},{3,4},{4,3},{5,6},{6,5},{7,8},{8,7},{9,10},{10,9},{11,... | collective-permute-start | bytes 503816 | tf_op jit(solution)/shard_map/ppermute | solution.py:425
  43.5 4.2 %collective-permute-start = (f32[328,128]{1,0:T(8,128)S(1)}, f32[328,128]{1,0:T(8,128)S(1)}, u32[]{:S(2)}, u32[]{:S(2)}) collective-permute-start(f32[328,128]{1,0:T(8,128)S(1)} %get-tuple-element.21.refs_1_.refs_0_.refs_8_), channel_id=1, source_target_pairs={{0,1},{1,0},{2,3},{3,2},{4,5},{5,4},{6,7},{7,6},{8,9},{9,8},{10,11... | collective-permute-start | bytes 503816 | tf_op jit(solution)/shard_map/ppermute | solution.py:424
  48.5 16.6 %collective-permute-start.3 = (f32[328,128]{1,0:T(8,128)S(1)}, f32[328,128]{1,0:T(8,128)S(1)}, u32[]{:S(2)}, u32[]{:S(2)}) collective-permute-start(f32[328,128]{1,0:T(8,128)S(1)} %get-tuple-element.30.refs_7_.refs_8_), channel_id=1, source_target_pairs={{1,2},{2,1},{3,4},{4,3},{5,6},{6,5},{7,8},{8,7},{9,10},{10,9},{11,... | collective-permute-start | bytes 503816 | tf_op jit(solution)/shard_map/ppermute | solution.py:425
  52.4 12.7 %collective-permute-start.2 = (f32[328,128]{1,0:T(8,128)S(1)}, f32[328,128]{1,0:T(8,128)S(1)}, u32[]{:S(2)}, u32[]{:S(2)}) collective-permute-start(f32[328,128]{1,0:T(8,128)S(1)} %get-tuple-element.30.refs_7_.refs_8_), channel_id=1, source_target_pairs={{0,1},{1,0},{2,3},{3,2},{4,5},{5,4},{6,7},{7,6},{8,9},{9,8},{10,11... | collective-permute-start | bytes 503816 | tf_op jit(solution)/shard_map/ppermute | solution.py:424
  65.7 8.5 %collective-permute-start.5 = (f32[328,128]{1,0:T(8,128)S(1)}, f32[328,128]{1,0:T(8,128)S(1)}, u32[]{:S(2)}, u32[]{:S(2)}) collective-permute-start(f32[328,128]{1,0:T(8,128)S(1)} %get-tuple-element.32.refs_0_.refs_1_), channel_id=1, source_target_pairs={{1,2},{2,1},{3,4},{4,3},{5,6},{6,5},{7,8},{8,7},{9,10},{10,9},{11,... | collective-permute-start | bytes 503816 | tf_op jit(solution)/shard_map/ppermute | solution.py:425
  69.3 4.8 %collective-permute-start.4 = (f32[328,128]{1,0:T(8,128)S(1)}, f32[328,128]{1,0:T(8,128)S(1)}, u32[]{:S(2)}, u32[]{:S(2)}) collective-permute-start(f32[328,128]{1,0:T(8,128)S(1)} %get-tuple-element.32.refs_0_.refs_1_), channel_id=1, source_target_pairs={{0,1},{1,0},{2,3},{3,2},{4,5},{5,4},{6,7},{7,6},{8,9},{9,8},{10,11... | collective-permute-start | bytes 503816 | tf_op jit(solution)/shard_map/ppermute | solution.py:424
  74.6 7.9 %collective-permute-start.7 = (f32[328,128]{1,0:T(8,128)S(1)}, f32[328,128]{1,0:T(8,128)S(1)}, u32[]{:S(2)}, u32[]{:S(2)}) collective-permute-start(f32[328,128]{1,0:T(8,128)S(1)} %get-tuple-element.34.refs_0_.refs_1_), channel_id=1, source_target_pairs={{1,2},{2,1},{3,4},{4,3},{5,6},{6,5},{7,8},{8,7},{9,10},{10,9},{11,... | collective-permute-start | bytes 503816 | tf_op jit(solution)/shard_map/ppermute | solution.py:425
  79.2 3.4 %collective-permute-start.6 = (f32[328,128]{1,0:T(8,128)S(1)}, f32[328,128]{1,0:T(8,128)S(1)}, u32[]{:S(2)}, u32[]{:S(2)}) collective-permute-start(f32[328,128]{1,0:T(8,128)S(1)} %get-tuple-element.34.refs_0_.refs_1_), channel_id=1, source_target_pairs={{0,1},{1,0},{2,3},{3,2},{4,5},{5,4},{6,7},{7,6},{8,9},{9,8},{10,11... | collective-permute-start | bytes 503816 | tf_op jit(solution)/shard_map/ppermute | solution.py:424

commit v2 on v1

--- a/solution.py
+++ b/solution.py
@@ -60,17 +60,22 @@
     out_ref, mean_out, wall_out, packed_out, speed_out, jac_out, radius_out,
     rows_ref, plane_ref
 ):
-    for cell in range(CELLS):
-        for c1 in range(C1):
-            cols = slice(c1 * LANES, (c1 + 1) * LANES)
-            for var in range(VARS):
-                for part in range(2):
+    for c1 in range(C1):
+        cols = slice(c1 * LANES, (c1 + 1) * LANES)
+        for var in range(VARS):
+            for part in range(2):
+                pair = harm_ref[0, part, var, :, cols]
+                for cell in range(CELLS):
                     row = h_row(part, var, cell) + c1
-                    rows_ref[row : row + 1, :] = harm_ref[0, part, var, cell : cell + 1, cols]
+                    rows_ref[row : row + 1, :] = pair[cell : cell + 1, :]
+            pair = mean_ref[var, :, cols]
+            for cell in range(CELLS):
                 row = m_row(var, cell) + c1
-                plane_ref[row : row + 1, :] = mean_ref[var, cell : cell + 1, cols]
+                plane_ref[row : row + 1, :] = pair[cell : cell + 1, :]
+        pair = wall_ref[:, cols].astype(jnp.float32)
+        for cell in range(CELLS):
             row = M_ROWS + cell * C1 + c1
-            plane_ref[row : row + 1, :] = wall_ref[cell : cell + 1, cols].astype(jnp.float32)
+            plane_ref[row : row + 1, :] = pair[cell : cell + 1, :]
     omega = OMEGA_BASE * freq_ref[0].astype(jnp.float32)
     rows_ref[H_ROWS:, :] = jnp.full((rows_ref.shape[0] - H_ROWS, LANES), omega, jnp.float32)
     turned = rows_ref[...].T
@@ -82,7 +87,7 @@
         for a in range(VARS):
             for b in range(VARS):
                 row = base + VARS * a + b
-                jac_out[row : row + 1, :] = jnp.broadcast_to(
+                jac_out[row : row + 1, :] = 0.5 * jnp.broadcast_to(
                     matrix_ref[a : a + 1, b : b + 1], (1, LANES)
                 )
     lane = lax.broadcasted_iota(jnp.int32, (8, LANES), 1)
@@ -128,7 +133,7 @@
     def cross_parts(center):
         above, below = beside(center)
         fourth = (up(center) + down(center)) - 4.0 * (above + below) + 12.0 * center
-        return (above - below) * 0.5, fourth
+        return above - below, fourth
 
     def apply_matrix(base, tiles):
         out = []
@@ -162,13 +167,13 @@
 
 def stress(left, right, index):
     a, b = STRESS_PAIRS[index]
-    return 0.5 * (left[a] * left[b] + right[a] * right[b])
+    return left[a] * left[b] + right[a] * right[b]
 
 
 def own_terms(own, mean_block, first, omega_ref, wall_ref, jac_ref, radius_ref):
     _, beside, cross_parts, apply_matrix = tile_tools(jac_ref)
     omega = splat(omega_ref, 0)
-    inv_radius = 1.0 / splat(radius_ref, 0)
+    half_inv_radius = 0.5 / splat(radius_ref, 0)
     rows = {}
     for cell in range(CELLS):
         wall = WALL_RATE * wall_ref[cell * C1 : (cell + 1) * C1, :]
@@ -193,14 +198,14 @@
 
         def grad_y(tile):
             above, below = beside(tile)
-            return (above - below) * 0.5
+            return (above - below) * 0.25
 
         s = [stress(*harm, index) for index in range(len(STRESS_PAIRS))]
         terms = [
             -grad_y(s[1]),
-            -grad_y(s[3]) - 2.0 * s[4] * inv_radius,
-            -grad_y(s[4]) + (s[3] - s[5]) * inv_radius,
-            -grad_y(s[7]) - s[8] * inv_radius,
+            -grad_y(s[3]) - 2.0 * s[4] * half_inv_radius,
+            -grad_y(s[4]) + (s[3] - s[5]) * half_inv_radius,
+            -grad_y(s[7]) - s[8] * half_inv_radius,
         ]
         for index, term in enumerate(terms):
             rows[f_row(index, cell)] = term
@@ -282,7 +287,7 @@
         at = 2 + cell
         for part in range(2):
             diffs = [
-                (mean[1][at + 1] * cells[at + 1] - mean[1][at - 1] * cells[at - 1]) * 0.5
+                mean[1][at + 1] * cells[at + 1] - mean[1][at - 1] * cells[at - 1]
                 for cells in harm[part]
             ]
             flux = apply_matrix(0, diffs)
@@ -298,13 +303,13 @@
                 stress(*[[cells[x] for cells in harm[part]] for part in range(2)], index)
                 for x in (at + 1, at - 1)
             ]
-            return (above - below) * 0.5
+            return (above - below) * 0.25
 
         terms = [
             total(near_term(f_row(i, cell)) - grad_x(index))
             for i, index in enumerate((0, 1, 2, 6))
         ]
-        flux = apply_matrix(0, [(cells[at + 1] - cells[at - 1]) * 0.5 for cells in mean])
+        flux = apply_matrix(0, [cells[at + 1] - cells[at - 1] for cells in mean])
         for var in range(VARS):
             row = m_row(var, cell)
             res = near_term(H_ROWS + row) - flux[var] - EPS_FOURTH * axial_fourth(mean[var], at)
@@ -346,15 +351,20 @@
         rows_ref[2 * j : 2 * j + 2, :] = arrived_ref[j, 0:2, :]
         rows_ref[NZ + 2 * j : NZ + 2 * j + 2, :] = arrived_ref[j, 2:4, :]
     turned = rows_ref[...].T
+
+    def pair(rows):
+        return jnp.concatenate([turned[row : row + 1, :] for row in rows], axis=0)
+
     for var in range(VARS):
-        for cell in range(CELLS):
-            for c1 in range(C1):
-                cols = slice(c1 * LANES, (c1 + 1) * LANES)
-                for part in range(2):
-                    row = h_row(part, var, cell) + c1
-                    harm_out[0, part, var, cell : cell + 1, cols] = turned[row : row + 1, :]
-                row = H_ROWS + m_row(var, cell) + c1
-                mean_out[var, cell : cell + 1, cols] = turned[row : row + 1, :]
+        for c1 in range(C1):
+            cols = slice(c1 * LANES, (c1 + 1) * LANES)
+            for part in range(2):
+                harm_out[0, part, var, :, cols] = pair(
+                    [h_row(part, var, cell) + c1 for cell in range(CELLS)]
+                )
+            mean_out[var, :, cols] = pair(
+                [H_ROWS + m_row(var, cell) + c1 for cell in range(CELLS)]
+            )
 
 
 def f32(*shape):

time: 111 us -> 111 us (level)
  no operation moved by 1% of the time
where the time goes in v2:
time: 111 us; the launch traced here: 109 us
  blocking collectives  70.2 us (63%)
  starting transfers between devices  26 us (23%)
  waiting for transfers between devices  5.89 us (5%)
  Pallas kernels  5.81 us (5%)
  between operations  1.42 us (1%)
    all_to_all x1, blocking collectives, shards(): arrived = lax.all_to_all(sends, 'harm', 0, 0, tiled=True)  34.5 us
    all_to_all x1, blocking collectives, shards(): back = lax.all_to_all(result, 'harm', 0, 0, tiled=True)  25.3 us
    ppermute x4, starting transfers between devices, beside(): chip = lax.ppermute(state, 'slab', chip_pairs)  18.4 us
    all_to_all x1, blocking collectives, shards(): speeds = lax.all_to_all(speed, 'slab', 0, 0, tiled=True)  10.3 us
    ppermute x4, starting transfers between devices, beside(): core = lax.ppermute(state, 'slab', core_pairs)  7.68 us
    ppermute x4, waiting for transfers between devices, beside(): chip = lax.ppermute(state, 'slab', chip_pairs)  5.88 us
    pallas_call x4, Pallas kernels, section(): pl.pallas_call(functools.partial(section_kernel, stage=stage, cell_count=...  2.38 us
  transfers between devices with their start and end apart: 8, of which 3 were waited for; matrix products, arithmetic and copies ran while one was open for 0% of the time, Pallas kernels for 1%

profile of v2, /device:TPU:7, one launch (start us, length us, event | category | flops | bytes accessed | tf_op | source)
XLA Modules:
  0.0 109.3 jit_solution(807312454593508393)
XLA Ops:
  1.3 1.3 %open.1 = (f32[32,4,384]{2,1,0:T(4,128)S(1)}, f32[160,128]{1,0:T(8,128)S(1)}, f32[32,128]{1,0:T(8,128)S(1)}, f32[8,128]{1,0:T(8,128)S(1)}, f32[16,1,128]{2,1,0:T...) custom-call(f32[1,2,5,2,2048]{4,3,2,1,0:T(2,128)} %harm_ref.1, f32[5,2,2048]{2,1,0:T(2,128)} %mean_ref.1, ...), custom_call_target="tpu_custom_call" | custom-call | tf_op jit(solution)/shard_map/open/pallas_call | solution.py:395
  2.6 34.5 %all_to_all.15.arrived_ref = f32[32,4,384]{2,1,0:T(4,128)S(1)} all-to-all(f32[32,4,384]{2,1,0:T(4,128)S(1)} %get-tuple-element.19), channel_id=1, replica_groups=mesh['harm'=32,'slab'=16] {'harm'}, dimensions={0} | all-to-all | bytes 393216 | tf_op jit(solution)/shard_map/all_to_all | solution.py:414
  37.1 0.1 unpack.1
  37.2 6.3 %collective-permute-start.1 = (f32[328,128]{1,0:T(8,128)S(1)}, f32[328,128]{1,0:T(8,128)S(1)}, u32[]{:S(2)}, u32[]{:S(2)}) collective-permute-start(f32[328,128]{1,0:T(8,128)S(1)} %get-tuple-element.21.refs_1_.refs_0_.refs_8_), channel_id=1, source_target_pairs={{1,2},{2,1},{3,4},{4,3},{5,6},{6,5},{7,8},{8,7},{9,10},{10,9},{11,... | collective-permute-start | bytes 503816 | tf_op jit(solution)/shard_map/ppermute | solution.py:435
  43.5 1.9 %collective-permute-start = (f32[328,128]{1,0:T(8,128)S(1)}, f32[328,128]{1,0:T(8,128)S(1)}, u32[]{:S(2)}, u32[]{:S(2)}) collective-permute-start(f32[328,128]{1,0:T(8,128)S(1)} %get-tuple-element.21.refs_1_.refs_0_.refs_8_), channel_id=1, source_target_pairs={{0,1},{1,0},{2,3},{3,2},{4,5},{5,4},{6,7},{7,6},{8,9},{9,8},{10,11... | collective-permute-start | bytes 503816 | tf_op jit(solution)/shard_map/ppermute | solution.py:434
  45.5 2.3 %collective-permute-done.1.refs_3_ = f32[328,128]{1,0:T(8,128)S(1)} collective-permute-done((f32[328,128]{1,0:T(8,128)S(1)}, f32[328,128]{1,0:T(8,128)S(1)}, u32[]{:S(2)}, u32[]{:S(2)}) %collective-permute-start.1) | collective-permute-done | bytes 167968 | tf_op jit(solution)/shard_map/ppermute | solution.py:435
  47.7 0.0 collective-permute-done.refs_2_
  47.7 0.7 shard_map.77
  48.5 3.9 %collective-permute-start.3 = (f32[328,128]{1,0:T(8,128)S(1)}, f32[328,128]{1,0:T(8,128)S(1)}, u32[]{:S(2)}, u32[]{:S(2)}) collective-permute-start(f32[328,128]{1,0:T(8,128)S(1)} %get-tuple-element.30.refs_7_.refs_8_), channel_id=1, source_target_pairs={{1,2},{2,1},{3,4},{4,3},{5,6},{6,5},{7,8},{8,7},{9,10},{10,9},{11,... | collective-permute-start | bytes 503816 | tf_op jit(solution)/shard_map/ppermute | solution.py:435
  52.4 1.9 %collective-permute-start.2 = (f32[328,128]{1,0:T(8,128)S(1)}, f32[328,128]{1,0:T(8,128)S(1)}, u32[]{:S(2)}, u32[]{:S(2)}) collective-permute-start(f32[328,128]{1,0:T(8,128)S(1)} %get-tuple-element.30.refs_7_.refs_8_), channel_id=1, source_target_pairs={{0,1},{1,0},{2,3},{3,2},{4,5},{5,4},{6,7},{7,6},{8,9},{9,8},{10,11... | collective-permute-start | bytes 503816 | tf_op jit(solution)/shard_map/ppermute | solution.py:434
  54.3 10.3 %all_to_all.16.refs_6_.refs_7_ = f32[16,1,128]{2,1,0:T(1,128)S(1)} all-to-all(f32[16,1,128]{2,1,0:T(1,128)S(1)} %get-tuple-element.29), channel_id=1, replica_groups=mesh['harm'=32,'slab'=16] {'slab'}, dimensions={0} | all-to-all | bytes 16384 | tf_op jit(solution)/shard_map/all_to_all | solution.py:425
  64.6 0.4 shard_map.78.refs_6_
  65.0 0.0 collective-permute-done.3.refs_10_
  65.0 0.0 collective-permute-done.2.refs_9_
  65.0 0.6 shard_map.79
  65.6 3.6 %collective-permute-start.5 = (f32[328,128]{1,0:T(8,128)S(1)}, f32[328,128]{1,0:T(8,128)S(1)}, u32[]{:S(2)}, u32[]{:S(2)}) collective-permute-start(f32[328,128]{1,0:T(8,128)S(1)} %get-tuple-element.32.refs_0_.refs_1_), channel_id=1, source_target_pairs={{1,2},{2,1},{3,4},{4,3},{5,6},{6,5},{7,8},{8,7},{9,10},{10,9},{11,... | collective-permute-start | bytes 503816 | tf_op jit(solution)/shard_map/ppermute | solution.py:435
  69.2 1.9 %collective-permute-start.4 = (f32[328,128]{1,0:T(8,128)S(1)}, f32[328,128]{1,0:T(8,128)S(1)}, u32[]{:S(2)}, u32[]{:S(2)}) collective-permute-start(f32[328,128]{1,0:T(8,128)S(1)} %get-tuple-element.32.refs_0_.refs_1_), channel_id=1, source_target_pairs={{0,1},{1,0},{2,3},{3,2},{4,5},{5,4},{6,7},{7,6},{8,9},{9,8},{10,11... | collective-permute-start | bytes 503816 | tf_op jit(solution)/shard_map/ppermute | solution.py:434
  71.2 0.4 shard_map.80.refs_6_
  71.5 2.5 %collective-permute-done.5.refs_3_ = f32[328,128]{1,0:T(8,128)S(1)} collective-permute-done((f32[328,128]{1,0:T(8,128)S(1)}, f32[328,128]{1,0:T(8,128)S(1)}, u32[]{:S(2)}, u32[]{:S(2)}) %collective-permute-start.5) | collective-permute-done | bytes 167968 | tf_op jit(solution)/shard_map/ppermute | solution.py:435
  74.0 0.0 collective-permute-done.4.refs_2_
  74.0 0.5 shard_map.81
  74.5 4.5 %collective-permute-start.7 = (f32[328,128]{1,0:T(8,128)S(1)}, f32[328,128]{1,0:T(8,128)S(1)}, u32[]{:S(2)}, u32[]{:S(2)}) collective-permute-start(f32[328,128]{1,0:T(8,128)S(1)} %get-tuple-element.34.refs_0_.refs_1_), channel_id=1, source_target_pairs={{1,2},{2,1},{3,4},{4,3},{5,6},{6,5},{7,8},{8,7},{9,10},{10,9},{11,... | collective-permute-start | bytes 503816 | tf_op jit(solution)/shard_map/ppermute | solution.py:435
  79.1 1.9 %collective-permute-start.6 = (f32[328,128]{1,0:T(8,128)S(1)}, f32[328,128]{1,0:T(8,128)S(1)}, u32[]{:S(2)}, u32[]{:S(2)}) collective-permute-start(f32[328,128]{1,0:T(8,128)S(1)} %get-tuple-element.34.refs_0_.refs_1_), channel_id=1, source_target_pairs={{0,1},{1,0},{2,3},{3,2},{4,5},{5,4},{6,7},{7,6},{8,9},{9,8},{10,11... | collective-permute-start | bytes 503816 | tf_op jit(solution)/shard_map/ppermute | solution.py:434
  81.0 0.4 shard_map.82.refs_6_
  81.4 1.1 collective-permute-done.7.refs_3_
  82.5 0.0 collective-permute-done.6.refs_2_
  82.5 0.6 shard_map.83
  83.1 25.3 %all_to_all.17.arrived_ref = f32[32,4,512]{2,1,0:T(4,128)S(1)} all-to-all(f32[32,4,512]{2,1,0:T(4,128)S(1)} %shard_map.83), channel_id=1, replica_groups=mesh['harm'=32,'slab'=16] {'harm'}, dimensions={0} | all-to-all | bytes 524288 | tf_op jit(solution)/shard_map/all_to_all | solution.py:478
  108.4 0.9 restore.1
Async XLA Ops:
  37.2 10.5 %collective-permute-start.1 = (f32[328,128]{1,0:T(8,128)S(1)}, f32[328,128]{1,0:T(8,128)S(1)}, u32[]{:S(2)}, u32[]{:S(2)}) collective-permute-start(f32[328,128]{1,0:T(8,128)S(1)} %get-tuple-element.21.refs_1_.refs_0_.refs_8_), channel_id=1, source_target_pairs={{1,2},{2,1},{3,4},{4,3},{5,6},{6,5},{7,8},{8,7},{9,10},{10,9},{11,... | collective-permute-start | bytes 503816 | tf_op jit(solution)/shard_map/ppermute | solution.py:435
  43.5 4.2 %collective-permute-start = (f32[328,128]{1,0:T(8,128)S(1)}, f32[328,128]{1,0:T(8,128)S(1)}, u32[]{:S(2)}, u32[]{:S(2)}) collective-permute-start(f32[328,128]{1,0:T(8,128)S(1)} %get-tuple-element.21.refs_1_.refs_0_.refs_8_), channel_id=1, source_target_pairs={{0,1},{1,0},{2,3},{3,2},{4,5},{5,4},{6,7},{7,6},{8,9},{9,8},{10,11... | collective-permute-start | bytes 503816 | tf_op jit(solution)/shard_map/ppermute | solution.py:434
  48.5 16.6 %collective-permute-start.3 = (f32[328,128]{1,0:T(8,128)S(1)}, f32[328,128]{1,0:T(8,128)S(1)}, u32[]{:S(2)}, u32[]{:S(2)}) collective-permute-start(f32[328,128]{1,0:T(8,128)S(1)} %get-tuple-element.30.refs_7_.refs_8_), channel_id=1, source_target_pairs={{1,2},{2,1},{3,4},{4,3},{5,6},{6,5},{7,8},{8,7},{9,10},{10,9},{11,... | collective-permute-start | bytes 503816 | tf_op jit(solution)/shard_map/ppermute | solution.py:435
  52.4 12.7 %collective-permute-start.2 = (f32[328,128]{1,0:T(8,128)S(1)}, f32[328,128]{1,0:T(8,128)S(1)}, u32[]{:S(2)}, u32[]{:S(2)}) collective-permute-start(f32[328,128]{1,0:T(8,128)S(1)} %get-tuple-element.30.refs_7_.refs_8_), channel_id=1, source_target_pairs={{0,1},{1,0},{2,3},{3,2},{4,5},{5,4},{6,7},{7,6},{8,9},{9,8},{10,11... | collective-permute-start | bytes 503816 | tf_op jit(solution)/shard_map/ppermute | solution.py:434
  65.6 8.5 %collective-permute-start.5 = (f32[328,128]{1,0:T(8,128)S(1)}, f32[328,128]{1,0:T(8,128)S(1)}, u32[]{:S(2)}, u32[]{:S(2)}) collective-permute-start(f32[328,128]{1,0:T(8,128)S(1)} %get-tuple-element.32.refs_0_.refs_1_), channel_id=1, source_target_pairs={{1,2},{2,1},{3,4},{4,3},{5,6},{6,5},{7,8},{8,7},{9,10},{10,9},{11,... | collective-permute-start | bytes 503816 | tf_op jit(solution)/shard_map/ppermute | solution.py:435
  69.2 4.8 %collective-permute-start.4 = (f32[328,128]{1,0:T(8,128)S(1)}, f32[328,128]{1,0:T(8,128)S(1)}, u32[]{:S(2)}, u32[]{:S(2)}) collective-permute-start(f32[328,128]{1,0:T(8,128)S(1)} %get-tuple-element.32.refs_0_.refs_1_), channel_id=1, source_target_pairs={{0,1},{1,0},{2,3},{3,2},{4,5},{5,4},{6,7},{7,6},{8,9},{9,8},{10,11... | collective-permute-start | bytes 503816 | tf_op jit(solution)/shard_map/ppermute | solution.py:434
  74.5 7.9 %collective-permute-start.7 = (f32[328,128]{1,0:T(8,128)S(1)}, f32[328,128]{1,0:T(8,128)S(1)}, u32[]{:S(2)}, u32[]{:S(2)}) collective-permute-start(f32[328,128]{1,0:T(8,128)S(1)} %get-tuple-element.34.refs_0_.refs_1_), channel_id=1, source_target_pairs={{1,2},{2,1},{3,4},{4,3},{5,6},{6,5},{7,8},{8,7},{9,10},{10,9},{11,... | collective-permute-start | bytes 503816 | tf_op jit(solution)/shard_map/ppermute | solution.py:435
  79.1 3.4 %collective-permute-start.6 = (f32[328,128]{1,0:T(8,128)S(1)}, f32[328,128]{1,0:T(8,128)S(1)}, u32[]{:S(2)}, u32[]{:S(2)}) collective-permute-start(f32[328,128]{1,0:T(8,128)S(1)} %get-tuple-element.34.refs_0_.refs_1_), channel_id=1, source_target_pairs={{0,1},{1,0},{2,3},{3,2},{4,5},{5,4},{6,7},{7,6},{8,9},{9,8},{10,11... | collective-permute-start | bytes 503816 | tf_op jit(solution)/shard_map/ppermute | solution.py:434
